TPU v7x, 32 devices: a whole 2x2x4 slice. The times are simulated.
32 devices in a mesh: mem: 4 (over y, x), cell: 8 (over z, core).
Axes of the slice: x: 2, y: 2, z: 4, core: 2. Of those that a mesh axis runs over, the one named last changes fastest.
Arguments:
- state: bfloat16 [16384, 40, 120], P('cell', 'mem'), may hold values from -6 to 6
- vertical_weight: bfloat16 [8192, 120], P('cell'), may hold values from -0.5 to 0.5
- horizontal_weight: float32 [8192, 4], P('cell'), may hold values from 0.05 to 0.45
- obs_slot: int32 [8192, 4], P('cell'), may hold values from 0 to 4095, as said below
- request_cell: int32 [8, 4096], P('cell'), may hold values from 0 to 2047
- obs_value: float32 [8192], P('cell'), may hold values from -6 to 6
- obs_error: float32 [8192], P('cell'), may hold values from 0.5 to 2
- obs_region: int32 [8192], P('cell'), may hold values from 0 to 63, as said below
Outputs:
- cov_matrix: float32 [64, 40, 40], P('cell', 'mem')
- innovation_proj: float32 [64, 40], P('cell', 'mem')
Inputs may be any that keep to these rules, and one draw needn't show every extreme that they name: `obs_slot`: within one owner's 1024 observations all 4096 slots differ, so every slot is used: 1024 ask the owner's own patch and 768 each of the four patches at distance 1 and 2. `obs_region`: an observation's region is one of the 8 regions of its owner's patch or of the patches just before or after it (indices wrap); patch p holds regions p * 8 to p * 8 + 7.
All inputs are finite; a program needn't handle non-finite values.
Results may differ from a plain program's by a relative error of at most 0.0003.
Values may be sent and summed in bfloat16 or wider, within the bound.
A program may use at most 128 MiB of HBM per device.

v0:
```python
import functools

import jax
import jax.numpy as jnp
from jax import lax
from jax.experimental import pallas as pl
from jax.experimental.pallas import tpu as pltpu
from jax.sharding import PartitionSpec as P

REG_DEV = 8
TILE = 256
MOVES = (-2, -1, 1, 2)
ANY = pl.BlockSpec(memory_space=pl.ANY)
MESH = pl.DeviceIdType.MESH
VMEM = pl.BlockSpec(memory_space=pltpu.VMEM)
NT = (((1,), (1,)), ((), ()))
f32, bf16, i32 = jnp.float32, jnp.bfloat16, jnp.int32


def split(x):
    top = x.astype(bf16).astype(f32)
    return top, x - top


def row16(row):
    return jnp.broadcast_to(row, (16, row.shape[1])).astype(bf16)


def onehot(row, count):
    lanes = row.shape[1]
    ids = lax.broadcasted_iota(i32, (count, lanes), 0).astype(f32).astype(bf16)
    hit = ids.reshape(count // 16, 16, lanes) == row16(row)[None]
    return jnp.where(hit, bf16(1), bf16(0)).reshape(count, lanes)


def spread_rows(row, value, count):
    ids = lax.broadcasted_iota(i32, (count, row.shape[1]), 0).astype(f32)
    return jnp.where(ids == row, value, 0.0)


def ring(axis, by):
    return lax.rem(lax.axis_index(axis) + by + lax.axis_size(axis), lax.axis_size(axis))


def remote(src, dst, send, recv, **target):
    return pltpu.make_async_remote_copy(
        src_ref=src,
        dst_ref=dst,
        send_sem=send,
        recv_sem=recv,
        device_id=target,
        device_id_type=MESH,
    )


def started(*args, **target):
    copy = remote(*args, **target)
    copy.start()
    return copy


def spread_sum(wheres, terms_of, count):
    total = None
    for where, terms in zip(wheres, terms_of):
        high = (where >> 8).astype(f32)
        left = jnp.concatenate([spread_rows(high, t, count) for t in terms], axis=0)
        part = lax.dot_general(
            left.astype(bf16),
            onehot((where & 255).astype(f32), TILE),
            NT,
            preferred_element_type=f32,
        )
        total = part if total is None else total + part
    return total


def bucket_at(turns, i):
    b = i32(0)
    for turn in turns:
        b += jnp.where(i >= turn, 1, 0)
    return b


def largest_divisor(n, most):
    return max(u for u in range(1, most + 1) if n % u == 0)


def kernel(
    own,
    halo,
    table_hbm,
    slot_hbm,
    h_hbm,
    w_hbm,
    state_hbm,
    value_hbm,
    error_hbm,
    region_hbm,
    cov_ref,
    proj_ref,
    table_ref,
    slot_ref,
    h_ref,
    wall_ref,
    state_ref,
    value_ref,
    error_ref,
    region_ref,
    cells,
    sent,
    got,
    sorted_ref,
    picked,
    wide,
    dots_ref,
    equiv,
    gathered,
    sums,
    shares,
    load_sem,
    cell_send,
    cell_recv,
    wall_send,
    wall_recv,
    note_send,
    note_recv,
    equiv_send,
    equiv_recv,
    sums_send,
    sums_recv,
):
    far = len(MOVES)
    chunks = own + far * halo
    levels, obs_dev = w_hbm.shape
    members = state_hbm.shape[0] // levels
    blocks = obs_dev // TILE
    buckets = state_hbm.shape[1] // TILE
    patches, sharers = lax.axis_size("cell"), lax.axis_size("mem")
    here, member = lax.axis_index("cell"), lax.axis_index("mem")
    share = obs_dev // sharers

    loads = []
    for number, (src, dst) in enumerate(
        (
            (table_hbm, table_ref),
            (w_hbm, wall_ref.at[:, :obs_dev]),
            (slot_hbm, slot_ref),
            (h_hbm, h_ref),
            (state_hbm, state_ref),
            (value_hbm, value_ref),
            (error_hbm, error_ref),
            (region_hbm, region_ref),
        )
    ):
        copy = pltpu.make_async_copy(src, dst, load_sem.at[number])
        copy.start()
        loads.append(copy)
    barrier = pltpu.get_barrier_semaphore()
    greeted = [(m, c) for m in range(sharers) for c in (0,) + MOVES if (m, c) != (0, 0)]
    for m, c in greeted:
        pl.semaphore_signal(
            barrier,
            inc=1,
            device_id={"mem": ring("mem", m), "cell": ring("cell", c)},
            device_id_type=MESH,
        )

    even = 1 - lax.rem(here, 2)
    outer = 1 - 2 * even
    offsets = (0, -outer, outer, 2 * outer, -2 * outer)
    asked = (0, -outer, outer, -2 * outer, 2 * outer)
    part_of = (0, 1 + even, 2 - even, 3 * even, 3 - 3 * even)
    cell_of = [ring("cell", by) for by in offsets]
    asked_of = [ring("cell", by) for by in asked]

    loads[0].wait()
    loads[1].wait()
    pl.semaphore_wait(barrier, len(greeted))

    def segment(k):
        return pl.ds(own + part_of[k] * halo, halo)

    def landing(k):
        return pl.ds(own + (k - 1) * halo, halo)

    first = [
        started(
            table_ref.at[segment(k)],
            cells.at[landing(k)],
            cell_send.at[k],
            cell_recv.at[k],
            cell=asked_of[k],
        )
        for k in range(1, 1 + far)
    ]
    mine = wall_ref.at[:, :obs_dev]
    heavy = [
        started(
            mine,
            wall_ref.at[:, k * obs_dev : (k + 1) * obs_dev],
            wall_send.at[k],
            wall_recv.at[k],
            cell=asked_of[k],
        )
        for k in range(1, far)
    ]

    loads[2].wait()
    loads[3].wait()
    lane = lax.broadcasted_iota(i32, (1, TILE), 1).astype(f32)
    wheres, terms_of = [], []
    for k in range(slot_ref.shape[0]):
        for j in range(blocks):
            tops, rest = split(h_ref[k : k + 1, j * TILE : (j + 1) * TILE])
            wheres.append(slot_ref[k : k + 1, j * TILE : (j + 1) * TILE])
            terms_of.append([jnp.full((1, TILE), float(j), f32), lane, tops, rest])
    by_slot = spread_sum(wheres, terms_of, chunks)
    slot_obs = by_slot[:chunks] * TILE + by_slot[chunks : 2 * chunks]
    slot_h = by_slot[2 * chunks : 3 * chunks] + by_slot[3 * chunks :]
    for c in range(chunks):
        sent[0, c] = slot_obs[c : c + 1]
        sent[1, c] = slot_h[c : c + 1]
    second = [
        started(
            sent.at[:, segment(k)],
            got.at[:, landing(k)],
            note_send.at[k],
            note_recv.at[k],
            cell=asked_of[k],
        )
        for k in range(1, 1 + far)
    ]

    for copy in first:
        copy.wait()
    cell_rows = [table_ref[c] if c < own else cells[c] for c in range(chunks)]
    bucket_ids = lax.broadcasted_iota(i32, (8, TILE), 0)
    member_of = jnp.concatenate(
        [jnp.where(bucket_ids == (row >> 8), 1.0, 0.0) for row in cell_rows], axis=0
    )
    rows = 8 * chunks
    place = lax.broadcasted_iota(i32, (TILE, TILE), 0) < lax.broadcasted_iota(i32, (TILE, TILE), 1)
    within = jnp.dot(
        member_of.astype(bf16), jnp.where(place, 1.0, 0.0).astype(bf16), preferred_element_type=f32
    )

    def order(axis):
        index = lax.broadcasted_iota(i32, (rows, rows), axis)
        chunk = index >> 3
        late = jnp.where(chunk >= own + halo, 1, 0)
        return (late * 8 + (index & 7)) * chunks + chunk

    before = jnp.where(order(1) < order(0), 1.0, 0.0).astype(bf16)
    ahead = jnp.dot(before, member_of.astype(bf16), preferred_element_type=f32)
    base = jnp.sum(ahead, axis=1, keepdims=True)
    position = jnp.sum(((within + base) * member_of).reshape(chunks, 8, TILE), axis=1)
    position = position.astype(i32)
    wheres = [position[c : c + 1] for c in range(chunks)]
    sorted_ref[: 2 * chunks] = spread_sum(
        wheres, [[(c & 255).astype(f32), (c >> 8).astype(f32)] for c in cell_rows], chunks
    )

    groups = [
        (0, own + halo, 0, 2 * blocks),
        (own + halo, chunks, 2 * blocks, (1 + far) * blocks),
    ]
    turns_of, starts, at = [], [], 0
    for low, high, _, _ in groups:
        turns = []
        for b in range(1, buckets):
            below = sum(jnp.where(row < b * TILE, 1, 0) for row in cell_rows[low:high])
            count = jnp.sum(below)
            turns.append(b + lax.shift_right_logical(jnp.maximum(count - 1, 0), 8))
        turns_of.append(turns)
        starts.append(at)
        at += high - low + buckets - 1
    loads[4].wait()
    for (low, high, _, _), turns, start in zip(groups, turns_of, starts):

        def pick(i, carry):
            b = bucket_at(turns, i)
            t = low + i - b
            held = sorted_ref[pl.ds(chunks + t, 1), :] == b.astype(f32)
            row = jnp.where(held, sorted_ref[pl.ds(t, 1), :], -1.0)
            picked[start + i] = jnp.dot(
                state_ref[:, pl.ds(b * TILE, TILE)],
                onehot(row, TILE),
                preferred_element_type=f32,
            )
            return carry

        steps = high - low + buckets - 1
        lax.fori_loop(0, steps, pick, 0, unroll=largest_divisor(steps, 8))

    for copy in second:
        copy.wait()
    terms_of = []
    for c in range(chunks):
        if c < own:
            source, obs, weight = 0, slot_obs[c : c + 1], slot_h[c : c + 1]
        else:
            source, obs, weight = 1 + (c - own) // halo, got[0, c], got[1, c]
        obs = obs.astype(i32)
        upper = ((obs >> 8) + source * blocks).astype(f32)
        terms_of.append([upper, (obs & 255).astype(f32), *split(weight)])
    sorted_ref[2 * chunks :] = spread_sum(wheres, terms_of, chunks)

    forward = None
    replies = []
    for number, ((low, high, near, end), turns, start) in enumerate(
        zip(groups, turns_of, starts)
    ):
        if number == 0:
            heavy[0].wait()
        else:
            heavy[1].wait()
            forward = started(
                wall_ref.at[:, 2 * obs_dev : 3 * obs_dev],
                wall_ref.at[:, 4 * obs_dev :],
                wall_send.at[4],
                wall_recv.at[4],
                cell=cell_of[1],
            )
            heavy[2].wait()
            forward.wait()

        def weigh(t, carry):
            upper = sorted_ref[pl.ds(2 * chunks + t, 1), :]
            lower = sorted_ref[pl.ds(3 * chunks + t, 1), :]
            total = jnp.zeros((levels, TILE), f32)
            for k in range(near, end):
                total += jnp.dot(
                    wall_ref[:, k * TILE : (k + 1) * TILE],
                    onehot(jnp.where(upper == k, lower, -1.0), TILE),
                    preferred_element_type=f32,
                )
            wide[t] = total
            return carry

        lax.fori_loop(low, high, weigh, 0, unroll=largest_divisor(high - low, 7))

        def reduce(i, carry):
            t = low + i - bucket_at(turns, i)
            columns = picked[start + i].reshape(members, levels, TILE)
            dots_ref[start + i, :members] = jnp.sum(columns * wide[t][None], axis=1)
            return carry

        steps = high - low + buckets - 1
        lax.fori_loop(0, steps, reduce, 0, unroll=largest_divisor(steps, 2))

        total = jnp.zeros(((end - near) * 32, TILE), f32)
        for t in range(low, high):
            upper = sorted_ref[2 * chunks + t : 2 * chunks + t + 1, :]
            lower = sorted_ref[3 * chunks + t : 3 * chunks + t + 1, :]
            weight = (
                sorted_ref[4 * chunks + t : 4 * chunks + t + 1, :]
                + sorted_ref[5 * chunks + t : 5 * chunks + t + 1, :]
            )
            dots = jnp.zeros((members, TILE), f32)
            for b in range(buckets):
                at = t - low + b
                here_b = (bucket_at(turns, at) == b).astype(i32).astype(f32)
                dots += here_b * dots_ref[start + at, :members]
            dots = jnp.concatenate(
                [dots * weight, jnp.zeros((16 - members, TILE), f32)], axis=0
            )
            both = jnp.concatenate(split(dots), axis=0).astype(bf16)
            key = row16(upper)[:1]
            left = jnp.concatenate(
                [jnp.where(key == bf16(k), both, bf16(0)) for k in range(near, end)], axis=0
            )
            total += lax.dot_general(left, onehot(lower, TILE), NT, preferred_element_type=f32)
        for k in range(near, end):
            at = (k - near) * 32
            piece = total[at : at + 16] + total[at + 16 : at + 32]
            source, lanes = k // blocks, k % blocks * TILE
            equiv[source, lanes // share, :, lanes % share : lanes % share + TILE] = piece[
                :members
            ]
        for source in range(near // blocks, end // blocks):
            for by in range(sharers):
                if source or by:
                    target = ring("mem", by)
                    replies.append(
                        started(
                            equiv.at[source, target],
                            gathered.at[source, member],
                            equiv_send.at[source * sharers + by],
                            equiv_recv.at[source * sharers + by],
                            mem=target,
                            cell=cell_of[source],
                        )
                    )

    for load in loads[5:]:
        load.wait()
    lanes = pl.ds(pl.multiple_of(member * share, 128), share)
    error = error_ref[:, lanes]
    inverse = 1.0 / (error * error)
    region = region_ref[:, lanes] - (here - 1) * REG_DEV
    region = jnp.where(region < 0, region + patches * REG_DEV, region)
    region = jnp.where(region >= patches * REG_DEV, region - patches * REG_DEV, region)
    gathered[0, member] = equiv[0, member]
    for copy in replies:
        copy.wait()
    whole = []
    for m in range(sharers):
        piece = gathered[0, m]
        for source in range(1, 1 + far):
            piece = piece + gathered[source, m]
        whole.append(piece)
    whole = jnp.concatenate(whole, axis=0)
    everyone = whole.shape[0]
    mean = jnp.sum(whole, axis=0, keepdims=True) * (1.0 / everyone)
    spread = whole - mean
    innov = value_ref[:, lanes] - mean
    right = jnp.concatenate([spread, innov], axis=0) * inverse
    width = sums.shape[-1] // 2
    blank = jnp.zeros((width - everyone - 1, share), f32)
    right = [jnp.concatenate([x, blank], axis=0) for x in split(right)]
    zero = jnp.zeros((width, share), f32)
    ids = lax.broadcasted_iota(i32, (REG_DEV, share), 0)
    hits = [ids + part * REG_DEV == region for part in range(3)]
    product = functools.partial(lax.dot_general, dimension_numbers=NT, preferred_element_type=f32)
    half = members // 2
    result = None
    for side in range(2):
        rights = [
            jnp.concatenate([x, zero] if side == 0 else [zero, x], axis=0).astype(bf16)
            for x in right
        ]
        lefts = []
        for piece in split(spread):
            lefts.append(
                jnp.concatenate(
                    [
                        jnp.where(hit, piece[at : at + 1], 0.0)
                        for m in range(sharers)
                        for hit in hits
                        for at in range(m * members + side * half, m * members + (side + 1) * half)
                    ],
                    axis=0,
                ).astype(bf16)
            )
        part = (
            product(lefts[0], rights[0])
            + product(lefts[0], rights[1])
            + product(lefts[1], rights[0])
        )
        result = part if result is None else result + part
    sums[...] = result.reshape(sums.shape)
    copies = []
    for by in range(sharers):
        target = ring("mem", by)
        for part in range(3):
            if by or part != 1:
                number = by * 3 + part
                copies.append(
                    started(
                        sums.at[target, part],
                        shares.at[member, part],
                        sums_send.at[number],
                        sums_recv.at[number],
                        mem=target,
                        cell=ring("cell", part - 1),
                    )
                )
    shares[member, 1] = sums[member, 1]
    for copy in copies:
        copy.wait()
    final = shares[0, 0]
    for m in range(sharers):
        for part in range(3):
            if m or part:
                final = final + shares[m, part]
    final = final.reshape(half, REG_DEV, 2 * width)
    cov_ref[:half] = final[:, :, :everyone]
    cov_ref[half:] = final[:, :, width : width + everyone]
    lanes = lax.broadcasted_iota(i32, (REG_DEV, members), 1)
    proj = jnp.zeros((REG_DEV, members), f32)
    for m in range(members):
        at = everyone + m // half * width
        proj = jnp.where(lanes == m, final[m % half, :, at : at + 1], proj)
    proj_ref[...] = proj


def on_device(
    state,
    vertical_weight,
    horizontal_weight,
    obs_slot,
    request_cell,
    obs_value,
    obs_error,
    obs_region,
):
    sharers = lax.axis_size("mem")
    cell_dev, members, levels = state.shape
    obs_dev, neigh = obs_slot.shape
    own = obs_dev // TILE
    halo = 3 * obs_dev // 4 // TILE
    far = len(MOVES)
    chunks = own + far * halo
    sources = 1 + far
    buckets = cell_dev // TILE
    steps = chunks + 2 * (buckets - 1)
    share = obs_dev // sharers
    everyone = sharers * members
    width = everyone + 1 + (-(everyone + 1)) % 16
    rows = members // 2 * REG_DEV
    dma = lambda n: pltpu.SemaphoreType.DMA((n,))
    cov, proj = pl.pallas_call(
        functools.partial(kernel, own, halo),
        out_shape=(
            jax.ShapeDtypeStruct((members, REG_DEV, everyone), f32),
            jax.ShapeDtypeStruct((REG_DEV, members), f32),
        ),
        in_specs=[ANY] * 8,
        out_specs=(VMEM, VMEM),
        scratch_shapes=[
            pltpu.VMEM((chunks, 1, TILE), i32),
            pltpu.VMEM((neigh, obs_dev), i32),
            pltpu.VMEM((neigh, obs_dev), f32),
            pltpu.VMEM((levels, sources * obs_dev), bf16),
            pltpu.VMEM((members * levels, cell_dev), bf16),
            pltpu.VMEM((1, obs_dev), f32),
            pltpu.VMEM((1, obs_dev), f32),
            pltpu.VMEM((1, obs_dev), i32),
            pltpu.VMEM((chunks, 1, TILE), i32),
            pltpu.VMEM((2, chunks, 1, TILE), f32),
            pltpu.VMEM((2, chunks, 1, TILE), f32),
            pltpu.VMEM((6 * chunks, TILE), f32),
            pltpu.VMEM((steps, members * levels, TILE), f32),
            pltpu.VMEM((chunks, levels, TILE), f32),
            pltpu.VMEM((steps, 16, TILE), f32),
            pltpu.VMEM((sources, sharers, members, share), f32),
            pltpu.VMEM((sources, sharers, members, share), f32),
            pltpu.VMEM((sharers, 3, rows, 2 * width), f32),
            pltpu.VMEM((sharers, 3, rows, 2 * width), f32),
            dma(8),
            dma(5),
            dma(5),
            dma(5),
            dma(5),
            dma(5),
            dma(5),
            dma(sources * sharers),
            dma(sources * sharers),
            dma(3 * sharers),
            dma(3 * sharers),
        ],
        compiler_params=pltpu.CompilerParams(
            collective_id=0, has_side_effects=True, vmem_limit_bytes=63 * 2**20
        ),
    )(
        request_cell.reshape(chunks, 1, TILE),
        obs_slot.T,
        horizontal_weight.T,
        vertical_weight.T,
        state.transpose(1, 2, 0).reshape(members * levels, cell_dev),
        obs_value.reshape(1, obs_dev),
        obs_error.reshape(1, obs_dev),
        obs_region.reshape(1, obs_dev),
    )
    return cov.transpose(1, 0, 2), proj


def solution(mesh):
    in_specs = (
        P("cell", "mem", None),
        P("cell", None),
        P("cell", None),
        P("cell", None),
        P("cell", None),
        P("cell"),
        P("cell"),
        P("cell"),
    )
    out_specs = (P("cell", "mem", None), P("cell", "mem"))
    return jax.shard_map(
        on_device, mesh=mesh, in_specs=in_specs, out_specs=out_specs, check_vma=False
    )
```

profile of v0, /device:TPU:0, one launch (start us, length us, event | category | flops | bytes accessed | tf_op | source)
XLA Modules:
  0.0 50.4 jit_solution(17038332359535920603)
XLA Ops:
  0.6 47.1 %shard_map.95 = (f32[10,8,40]{2,1,0:T(8,128)}, f32[8,10]{1,0:T(8,128)}) custom-call(s32[16,1,256]{2,1,0:T(1,128)} %bitcast.14, s32[4,1024]{1,0:T(4,128)} %bitcast.15, f32[4,1024]{1,0:T(4,128)} %bitcast.16, bf16[120,1024]{1,0:T(8,128)(2,1)} %bitcast.12, bf16[1200,2048]{1,0:T(8,128)(2,1)} %bitcast.11, f32[1,1024]{1,0:T(1,128)} %bitcast.17, ...), custom_call_target="tpu_custom_call" | custom-call | tf_op jit(solution)/shard_map/pallas_call | solution.py:512
  47.8 1.4 %copy.12 = f32[8,10,40]{2,0,1:T(8,128)} copy(f32[8,10,40]{2,0,1:T(8,128)} %bitcast.13) | data formatting | bytes 25600
  49.2 1.3 %copy.13 = f32[8,10]{1,0:T(8,128)} copy(f32[8,10]{1,0:T(8,128)} %get-tuple-element.9) | data formatting | bytes 640
where the time goes:
time: 50.7 us; the launch traced here: 50.4 us
  Pallas kernels  47.1 us (93%)
  local copies, waits for them, and re-layouts  2.67 us (5%)
  between operations  0.64 us (1%)
    pallas_call x1, Pallas kernels, on_device(): pl.pallas_call(functools.partial(kernel, own, halo), out_shape=(jax.Shape...  47.1 us
    unnamed x2, local copies, waits for them, and re-layouts  2.67 us

commit v1 on v0

--- a/solution.py
+++ b/solution.py
@@ -10,7 +10,7 @@
 REG_DEV = 8
 TILE = 256
 MOVES = (-2, -1, 1, 2)
-ANY = pl.BlockSpec(memory_space=pl.ANY)
+HBM = pl.BlockSpec(memory_space=pltpu.HBM)
 MESH = pl.DeviceIdType.MESH
 VMEM = pl.BlockSpec(memory_space=pltpu.VMEM)
 NT = (((1,), (1,)), ((), ()))
@@ -96,8 +96,7 @@
     value_hbm,
     error_hbm,
     region_hbm,
-    cov_ref,
-    proj_ref,
+    out_ref,
     table_ref,
     slot_ref,
     h_ref,
@@ -110,7 +109,6 @@
     sent,
     got,
     sorted_ref,
-    picked,
     wide,
     dots_ref,
     equiv,
@@ -122,6 +120,8 @@
     cell_recv,
     wall_send,
     wall_recv,
+    pass_send,
+    pass_recv,
     note_send,
     note_recv,
     equiv_send,
@@ -173,38 +173,6 @@
     cell_of = [ring("cell", by) for by in offsets]
     asked_of = [ring("cell", by) for by in asked]
 
-    loads[0].wait()
-    loads[1].wait()
-    pl.semaphore_wait(barrier, len(greeted))
-
-    def segment(k):
-        return pl.ds(own + part_of[k] * halo, halo)
-
-    def landing(k):
-        return pl.ds(own + (k - 1) * halo, halo)
-
-    first = [
-        started(
-            table_ref.at[segment(k)],
-            cells.at[landing(k)],
-            cell_send.at[k],
-            cell_recv.at[k],
-            cell=asked_of[k],
-        )
-        for k in range(1, 1 + far)
-    ]
-    mine = wall_ref.at[:, :obs_dev]
-    heavy = [
-        started(
-            mine,
-            wall_ref.at[:, k * obs_dev : (k + 1) * obs_dev],
-            wall_send.at[k],
-            wall_recv.at[k],
-            cell=asked_of[k],
-        )
-        for k in range(1, far)
-    ]
-
     loads[2].wait()
     loads[3].wait()
     lane = lax.broadcasted_iota(i32, (1, TILE), 1).astype(f32)
@@ -220,6 +188,26 @@
     for c in range(chunks):
         sent[0, c] = slot_obs[c : c + 1]
         sent[1, c] = slot_h[c : c + 1]
+    loads[0].wait()
+    loads[1].wait()
+    pl.semaphore_wait(barrier, len(greeted))
+
+    def segment(k):
+        return pl.ds(own + part_of[k] * halo, halo)
+
+    def landing(k):
+        return pl.ds(own + (k - 1) * halo, halo)
+
+    first = [
+        started(
+            table_ref.at[segment(k)],
+            cells.at[landing(k)],
+            cell_send.at[k],
+            cell_recv.at[k],
+            cell=asked_of[k],
+        )
+        for k in range(1, 1 + far)
+    ]
     second = [
         started(
             sent.at[:, segment(k)],
@@ -231,6 +219,22 @@
         for k in range(1, 1 + far)
     ]
 
+    def quarter(k):
+        return wall_ref.at[:, pl.ds(pl.multiple_of(k * obs_dev + member * share, 128), share)]
+
+    def whole_wall(k):
+        return wall_ref.at[:, k * obs_dev : (k + 1) * obs_dev]
+
+    outward = started(
+        quarter(0), quarter(2), wall_send.at[2], wall_recv.at[2], cell=asked_of[2]
+    )
+    near_wall = started(
+        whole_wall(0), whole_wall(1), wall_send.at[1], wall_recv.at[1], cell=asked_of[1]
+    )
+    inward = started(
+        whole_wall(0), whole_wall(3), wall_send.at[3], wall_recv.at[3], cell=asked_of[3]
+    )
+
     for copy in first:
         copy.wait()
     cell_rows = [table_ref[c] if c < own else cells[c] for c in range(chunks)]
@@ -255,10 +259,32 @@
     base = jnp.sum(ahead, axis=1, keepdims=True)
     position = jnp.sum(((within + base) * member_of).reshape(chunks, 8, TILE), axis=1)
     position = position.astype(i32)
+    for copy in second:
+        copy.wait()
+    terms_of = []
+    for c, cell in enumerate(cell_rows):
+        if c < own:
+            source, obs, weight = 0, slot_obs[c : c + 1], slot_h[c : c + 1]
+        else:
+            source, obs, weight = 1 + (c - own) // halo, got[0, c], got[1, c]
+        obs = obs.astype(i32)
+        terms_of.append(
+            [
+                (cell & 255).astype(f32),
+                (cell >> 8).astype(f32),
+                ((obs >> 8) + source * blocks).astype(f32),
+                (obs & 255).astype(f32),
+                *split(weight),
+            ]
+        )
     wheres = [position[c : c + 1] for c in range(chunks)]
-    sorted_ref[: 2 * chunks] = spread_sum(
-        wheres, [[(c & 255).astype(f32), (c >> 8).astype(f32)] for c in cell_rows], chunks
-    )
+    sorted_ref[...] = spread_sum(wheres, terms_of, chunks)
+
+    outward.wait()
+    passed = [
+        started(quarter(2), quarter(2), pass_send.at[by], pass_recv.at[by], mem=ring("mem", by))
+        for by in range(1, sharers)
+    ]
 
     groups = [
         (0, own + halo, 0, 2 * blocks),
@@ -275,35 +301,24 @@
         starts.append(at)
         at += high - low + buckets - 1
     loads[4].wait()
-    for (low, high, _, _), turns, start in zip(groups, turns_of, starts):
-
-        def pick(i, carry):
-            b = bucket_at(turns, i)
-            t = low + i - b
-            held = sorted_ref[pl.ds(chunks + t, 1), :] == b.astype(f32)
-            row = jnp.where(held, sorted_ref[pl.ds(t, 1), :], -1.0)
-            picked[start + i] = jnp.dot(
-                state_ref[:, pl.ds(b * TILE, TILE)],
-                onehot(row, TILE),
+    def weigh(t, near, end, more):
+        upper = sorted_ref[pl.ds(2 * chunks + t, 1), :]
+        lower = sorted_ref[pl.ds(3 * chunks + t, 1), :]
+        total = wide[t] if more else jnp.zeros((levels, TILE), f32)
+        for k in range(near, end):
+            total += jnp.dot(
+                wall_ref[:, k * TILE : (k + 1) * TILE],
+                onehot(jnp.where(upper == k, lower, -1.0), TILE),
                 preferred_element_type=f32,
             )
+        wide[t] = total
+
+    def weigh_all(low, high, near, end, more=False):
+        def body(t, carry):
+            weigh(t, near, end, more)
             return carry
 
-        steps = high - low + buckets - 1
-        lax.fori_loop(0, steps, pick, 0, unroll=largest_divisor(steps, 8))
-
-    for copy in second:
-        copy.wait()
-    terms_of = []
-    for c in range(chunks):
-        if c < own:
-            source, obs, weight = 0, slot_obs[c : c + 1], slot_h[c : c + 1]
-        else:
-            source, obs, weight = 1 + (c - own) // halo, got[0, c], got[1, c]
-        obs = obs.astype(i32)
-        upper = ((obs >> 8) + source * blocks).astype(f32)
-        terms_of.append([upper, (obs & 255).astype(f32), *split(weight)])
-    sorted_ref[2 * chunks :] = spread_sum(wheres, terms_of, chunks)
+        lax.fori_loop(low, high, body, 0, unroll=largest_divisor(high - low, 9))
 
     forward = None
     replies = []
@@ -311,42 +326,33 @@
         zip(groups, turns_of, starts)
     ):
         if number == 0:
-            heavy[0].wait()
+            near_wall.wait()
+            weigh_all(low, high, near, end)
         else:
-            heavy[1].wait()
-            forward = started(
-                wall_ref.at[:, 2 * obs_dev : 3 * obs_dev],
-                wall_ref.at[:, 4 * obs_dev :],
-                wall_send.at[4],
-                wall_recv.at[4],
-                cell=cell_of[1],
-            )
-            heavy[2].wait()
+            inward.wait()
+            weigh_all(low, high, near, end - blocks)
             forward.wait()
-
-        def weigh(t, carry):
-            upper = sorted_ref[pl.ds(2 * chunks + t, 1), :]
-            lower = sorted_ref[pl.ds(3 * chunks + t, 1), :]
-            total = jnp.zeros((levels, TILE), f32)
-            for k in range(near, end):
-                total += jnp.dot(
-                    wall_ref[:, k * TILE : (k + 1) * TILE],
-                    onehot(jnp.where(upper == k, lower, -1.0), TILE),
-                    preferred_element_type=f32,
-                )
-            wide[t] = total
-            return carry
-
-        lax.fori_loop(low, high, weigh, 0, unroll=largest_divisor(high - low, 7))
-
-        def reduce(i, carry):
-            t = low + i - bucket_at(turns, i)
-            columns = picked[start + i].reshape(members, levels, TILE)
+            weigh_all(low, high, end - blocks, end, more=True)
+
+        def pick(i, carry):
+            b = bucket_at(turns, i)
+            t = low + i - b
+            held = sorted_ref[pl.ds(chunks + t, 1), :] == b.astype(f32)
+            row = jnp.where(held, sorted_ref[pl.ds(t, 1), :], -1.0)
+            columns = jnp.dot(
+                state_ref[:, pl.ds(b * TILE, TILE)], onehot(row, TILE), preferred_element_type=f32
+            ).reshape(members, levels, TILE)
             dots_ref[start + i, :members] = jnp.sum(columns * wide[t][None], axis=1)
             return carry
 
         steps = high - low + buckets - 1
-        lax.fori_loop(0, steps, reduce, 0, unroll=largest_divisor(steps, 2))
+        lax.fori_loop(0, steps, pick, 0, unroll=largest_divisor(steps, 8))
+        if number == 0:
+            for copy in passed:
+                copy.wait()
+            forward = started(
+                whole_wall(2), whole_wall(4), wall_send.at[4], wall_recv.at[4], cell=cell_of[1]
+            )
 
         total = jnp.zeros(((end - near) * 32, TILE), f32)
         for t in range(low, high):
@@ -473,7 +479,14 @@
         for part in range(3):
             if m or part:
                 final = final + shares[m, part]
-    final = final.reshape(half, REG_DEV, 2 * width)
+    out_ref[...] = final
+
+
+def unpack_kernel(everyone, final_ref, cov_ref, proj_ref):
+    width = final_ref.shape[1] // 2
+    half = final_ref.shape[0] // REG_DEV
+    members = 2 * half
+    final = final_ref[...].reshape(half, REG_DEV, 2 * width)
     cov_ref[:half] = final[:, :, :everyone]
     cov_ref[half:] = final[:, :, width : width + everyone]
     lanes = lax.broadcasted_iota(i32, (REG_DEV, members), 1)
@@ -509,14 +522,11 @@
     width = everyone + 1 + (-(everyone + 1)) % 16
     rows = members // 2 * REG_DEV
     dma = lambda n: pltpu.SemaphoreType.DMA((n,))
-    cov, proj = pl.pallas_call(
+    final = pl.pallas_call(
         functools.partial(kernel, own, halo),
-        out_shape=(
-            jax.ShapeDtypeStruct((members, REG_DEV, everyone), f32),
-            jax.ShapeDtypeStruct((REG_DEV, members), f32),
-        ),
-        in_specs=[ANY] * 8,
-        out_specs=(VMEM, VMEM),
+        out_shape=jax.ShapeDtypeStruct((rows, 2 * width), f32),
+        in_specs=[HBM] * 8,
+        out_specs=VMEM,
         scratch_shapes=[
             pltpu.VMEM((chunks, 1, TILE), i32),
             pltpu.VMEM((neigh, obs_dev), i32),
@@ -530,7 +540,6 @@
             pltpu.VMEM((2, chunks, 1, TILE), f32),
             pltpu.VMEM((2, chunks, 1, TILE), f32),
             pltpu.VMEM((6 * chunks, TILE), f32),
-            pltpu.VMEM((steps, members * levels, TILE), f32),
             pltpu.VMEM((chunks, levels, TILE), f32),
             pltpu.VMEM((steps, 16, TILE), f32),
             pltpu.VMEM((sources, sharers, members, share), f32),
@@ -542,6 +551,8 @@
             dma(5),
             dma(5),
             dma(5),
+            dma(sharers),
+            dma(sharers),
             dma(5),
             dma(5),
             dma(sources * sharers),
@@ -550,7 +561,7 @@
             dma(3 * sharers),
         ],
         compiler_params=pltpu.CompilerParams(
-            collective_id=0, has_side_effects=True, vmem_limit_bytes=63 * 2**20
+            collective_id=0, has_side_effects=True, vmem_limit_bytes=60 * 2**20
         ),
     )(
         request_cell.reshape(chunks, 1, TILE),
@@ -562,6 +573,15 @@
         obs_error.reshape(1, obs_dev),
         obs_region.reshape(1, obs_dev),
     )
+    cov, proj = pl.pallas_call(
+        functools.partial(unpack_kernel, everyone),
+        out_shape=(
+            jax.ShapeDtypeStruct((members, REG_DEV, everyone), f32),
+            jax.ShapeDtypeStruct((REG_DEV, members), f32),
+        ),
+        in_specs=[VMEM],
+        out_specs=(VMEM, VMEM),
+    )(final)
     return cov.transpose(1, 0, 2), proj
 
 

time: 50.7 us -> 40.2 us (0.79)
  Pallas kernels: 47.1 us -> 39.3 us
  local copies, waits for them, and re-layouts: 2.67 us -> 0 us
    pallas_call x1 -> x2, Pallas kernels: 47.1 us -> 39.3 us  [the longest x1 37.9 us: on_device(): pl.pallas_call(functools.partial(kernel, own, halo), out_shape=jax.ShapeD...]
    unnamed x2 -> x0, local copies, waits for them, and re-layouts: 2.67 us -> none
where the time goes in v1:
time: 40.2 us; the launch traced here: 40 us
  Pallas kernels  39.3 us (98%)
  between operations  0.64 us (2%)
    pallas_call x1, Pallas kernels, on_device(): pl.pallas_call(functools.partial(kernel, own, halo), out_shape=jax.ShapeD...  37.9 us
    pallas_call x1, Pallas kernels, on_device(): pl.pallas_call(functools.partial(unpack_kernel, everyone), out_shape=(jax...  1.43 us

profile of v1, /device:TPU:0, one launch (start us, length us, event | category | flops | bytes accessed | tf_op | source)
XLA Modules:
  0.0 40.0 jit_solution(5438642932029603103)
XLA Ops:
  0.6 37.9 %shard_map.95.final_ref = f32[40,96]{1,0:T(8,128)} custom-call(s32[16,1,256]{2,1,0:T(1,128)} %bitcast.13, s32[4,1024]{1,0:T(4,128)} %bitcast.14, f32[4,1024]{1,0:T(4,128)} %bitcast.15, bf16[120,1024]{1,0:T(8,128)(2,1)} %bitcast.12, bf16[1200,2048]{1,0:T(8,128)(2,1)} %bitcast.11, f32[1,1024]{1,0:T(1,128)} %bitcast.16, f32[1,1024]{1,0:T(1,128)} %bitcast.17, ...), custom_call_target="tpu_custom_call" | custom-call | tf_op jit(solution)/shard_map/pallas_call | solution.py:525
  38.6 1.4 %shard_map.96 = (f32[10,8,40]{2,1,0:T(8,128)}, f32[8,10]{1,0:T(8,128)}) custom-call(f32[40,96]{1,0:T(8,128)} %shard_map.95.final_ref), custom_call_target="tpu_custom_call" | custom-call | tf_op jit(solution)/shard_map/pallas_call | solution.py:576

commit v2 on v1

--- a/solution.py
+++ b/solution.py
@@ -156,7 +156,7 @@
         copy.start()
         loads.append(copy)
     barrier = pltpu.get_barrier_semaphore()
-    greeted = [(m, c) for m in range(sharers) for c in (0,) + MOVES if (m, c) != (0, 0)]
+    greeted = [(0, c) for c in MOVES] + [(m, 0) for m in range(1, sharers)]
     for m, c in greeted:
         pl.semaphore_signal(
             barrier,
@@ -354,6 +354,8 @@
                 whole_wall(2), whole_wall(4), wall_send.at[4], wall_recv.at[4], cell=cell_of[1]
             )
 
+    for number in (1, 0):
+        (low, high, near, end), turns, start = groups[number], turns_of[number], starts[number]
         total = jnp.zeros(((end - near) * 32, TILE), f32)
         for t in range(low, high):
             upper = sorted_ref[2 * chunks + t : 2 * chunks + t + 1, :]
@@ -379,10 +381,12 @@
         for k in range(near, end):
             at = (k - near) * 32
             piece = total[at : at + 16] + total[at + 16 : at + 32]
-            source, lanes = k // blocks, k % blocks * TILE
-            equiv[source, lanes // share, :, lanes % share : lanes % share + TILE] = piece[
-                :members
-            ]
+            source, block = k // blocks, k % blocks * (TILE // 128)
+            for part in range(TILE // 128):
+                row = (block + part) % (share // 128) * members
+                equiv[source, (block + part) // (share // 128), row : row + members] = piece[
+                    :members, part * 128 : (part + 1) * 128
+                ]
         for source in range(near // blocks, end // blocks):
             for by in range(sharers):
                 if source or by:
@@ -414,7 +418,8 @@
         piece = gathered[0, m]
         for source in range(1, 1 + far):
             piece = piece + gathered[source, m]
-        whole.append(piece)
+        piece = [piece[at : at + members] for at in range(0, piece.shape[0], members)]
+        whole.append(jnp.concatenate(piece, axis=1))
     whole = jnp.concatenate(whole, axis=0)
     everyone = whole.shape[0]
     mean = jnp.sum(whole, axis=0, keepdims=True) * (1.0 / everyone)
@@ -542,8 +547,8 @@
             pltpu.VMEM((6 * chunks, TILE), f32),
             pltpu.VMEM((chunks, levels, TILE), f32),
             pltpu.VMEM((steps, 16, TILE), f32),
-            pltpu.VMEM((sources, sharers, members, share), f32),
-            pltpu.VMEM((sources, sharers, members, share), f32),
+            pltpu.VMEM((sources, sharers, members * share // 128, 128), f32),
+            pltpu.VMEM((sources, sharers, members * share // 128, 128), f32),
             pltpu.VMEM((sharers, 3, rows, 2 * width), f32),
             pltpu.VMEM((sharers, 3, rows, 2 * width), f32),
             dma(8),

time: 40.2 us -> 37.4 us (0.930)
  Pallas kernels: 39.3 us -> 36.6 us
    pallas_call x1, Pallas kernels: 37.9 us -> 35.1 us  [on_device(): pl.pallas_call(functools.partial(kernel, own, halo), out_shape=jax.ShapeD...]
where the time goes in v2:
time: 37.4 us; the launch traced here: 37.2 us
  Pallas kernels  36.6 us (98%)
  between operations  0.64 us (2%)
    pallas_call x1, Pallas kernels, on_device(): pl.pallas_call(functools.partial(kernel, own, halo), out_shape=jax.ShapeD...  35.1 us
    pallas_call x1, Pallas kernels, on_device(): pl.pallas_call(functools.partial(unpack_kernel, everyone), out_shape=(jax...  1.43 us

profile of v2, /device:TPU:0, one launch (start us, length us, event | category | flops | bytes accessed | tf_op | source)
XLA Modules:
  0.0 37.2 jit_solution(9770771051581334090)
XLA Ops:
  0.6 35.1 %shard_map.95.final_ref = f32[40,96]{1,0:T(8,128)} custom-call(s32[16,1,256]{2,1,0:T(1,128)} %bitcast.13, s32[4,1024]{1,0:T(4,128)} %bitcast.14, f32[4,1024]{1,0:T(4,128)} %bitcast.15, bf16[120,1024]{1,0:T(8,128)(2,1)} %bitcast.12, bf16[1200,2048]{1,0:T(8,128)(2,1)} %bitcast.11, f32[1,1024]{1,0:T(1,128)} %bitcast.16, f32[1,1024]{1,0:T(1,128)} %bitcast.17, ...), custom_call_target="tpu_custom_call" | custom-call | tf_op jit(solution)/shard_map/pallas_call | solution.py:530
  35.8 1.4 %shard_map.96 = (f32[10,8,40]{2,1,0:T(8,128)}, f32[8,10]{1,0:T(8,128)}) custom-call(f32[40,96]{1,0:T(8,128)} %shard_map.95.final_ref), custom_call_target="tpu_custom_call" | custom-call | tf_op jit(solution)/shard_map/pallas_call | solution.py:581

commit v3 on v2

--- a/solution.py
+++ b/solution.py
@@ -167,9 +167,9 @@
 
     even = 1 - lax.rem(here, 2)
     outer = 1 - 2 * even
-    offsets = (0, -outer, outer, 2 * outer, -2 * outer)
-    asked = (0, -outer, outer, -2 * outer, 2 * outer)
-    part_of = (0, 1 + even, 2 - even, 3 * even, 3 - 3 * even)
+    offsets = (0, -outer, 2 * outer, outer, -2 * outer)
+    asked = (0, -outer, -2 * outer, outer, 2 * outer)
+    part_of = (0, 1 + even, 3 * even, 2 - even, 3 - 3 * even)
     cell_of = [ring("cell", by) for by in offsets]
     asked_of = [ring("cell", by) for by in asked]
 
@@ -226,13 +226,13 @@
         return wall_ref.at[:, k * obs_dev : (k + 1) * obs_dev]
 
     outward = started(
-        quarter(0), quarter(2), wall_send.at[2], wall_recv.at[2], cell=asked_of[2]
+        quarter(0), quarter(3), wall_send.at[3], wall_recv.at[3], cell=asked_of[3]
     )
     near_wall = started(
         whole_wall(0), whole_wall(1), wall_send.at[1], wall_recv.at[1], cell=asked_of[1]
     )
     inward = started(
-        whole_wall(0), whole_wall(3), wall_send.at[3], wall_recv.at[3], cell=asked_of[3]
+        whole_wall(0), whole_wall(2), wall_send.at[2], wall_recv.at[2], cell=asked_of[2]
     )
 
     for copy in first:
@@ -251,7 +251,7 @@
     def order(axis):
         index = lax.broadcasted_iota(i32, (rows, rows), axis)
         chunk = index >> 3
-        late = jnp.where(chunk >= own + halo, 1, 0)
+        late = jnp.where(chunk >= own + halo, 1, 0) + jnp.where(chunk >= own + 2 * halo, 1, 0)
         return (late * 8 + (index & 7)) * chunks + chunk
 
     before = jnp.where(order(1) < order(0), 1.0, 0.0).astype(bf16)
@@ -282,13 +282,14 @@
 
     outward.wait()
     passed = [
-        started(quarter(2), quarter(2), pass_send.at[by], pass_recv.at[by], mem=ring("mem", by))
+        started(quarter(3), quarter(3), pass_send.at[by], pass_recv.at[by], mem=ring("mem", by))
         for by in range(1, sharers)
     ]
 
     groups = [
         (0, own + halo, 0, 2 * blocks),
-        (own + halo, chunks, 2 * blocks, (1 + far) * blocks),
+        (own + halo, own + 2 * halo, 2 * blocks, 3 * blocks),
+        (own + 2 * halo, chunks, 3 * blocks, (1 + far) * blocks),
     ]
     turns_of, starts, at = [], [], 0
     for low, high, _, _ in groups:
@@ -320,41 +321,9 @@
 
         lax.fori_loop(low, high, body, 0, unroll=largest_divisor(high - low, 9))
 
-    forward = None
     replies = []
-    for number, ((low, high, near, end), turns, start) in enumerate(
-        zip(groups, turns_of, starts)
-    ):
-        if number == 0:
-            near_wall.wait()
-            weigh_all(low, high, near, end)
-        else:
-            inward.wait()
-            weigh_all(low, high, near, end - blocks)
-            forward.wait()
-            weigh_all(low, high, end - blocks, end, more=True)
-
-        def pick(i, carry):
-            b = bucket_at(turns, i)
-            t = low + i - b
-            held = sorted_ref[pl.ds(chunks + t, 1), :] == b.astype(f32)
-            row = jnp.where(held, sorted_ref[pl.ds(t, 1), :], -1.0)
-            columns = jnp.dot(
-                state_ref[:, pl.ds(b * TILE, TILE)], onehot(row, TILE), preferred_element_type=f32
-            ).reshape(members, levels, TILE)
-            dots_ref[start + i, :members] = jnp.sum(columns * wide[t][None], axis=1)
-            return carry
-
-        steps = high - low + buckets - 1
-        lax.fori_loop(0, steps, pick, 0, unroll=largest_divisor(steps, 8))
-        if number == 0:
-            for copy in passed:
-                copy.wait()
-            forward = started(
-                whole_wall(2), whole_wall(4), wall_send.at[4], wall_recv.at[4], cell=cell_of[1]
-            )
-
-    for number in (1, 0):
+
+    def answer(number):
         (low, high, near, end), turns, start = groups[number], turns_of[number], starts[number]
         total = jnp.zeros(((end - near) * 32, TILE), f32)
         for t in range(low, high):
@@ -401,6 +370,50 @@
                             cell=cell_of[source],
                         )
                     )
+
+    forward = None
+    for number, ((low, high, near, end), turns, start) in enumerate(
+        zip(groups, turns_of, starts)
+    ):
+        if number == 0:
+            near_wall.wait()
+            weigh_all(low, high, near, end)
+        elif number == 1:
+            inward.wait()
+            weigh_all(low, high, near, end)
+        else:
+            weigh_all(low, high, near, end - blocks)
+            forward.wait()
+            weigh_all(low, high, end - blocks, end, more=True)
+
+        def pick(i, carry):
+            b = bucket_at(turns, i)
+            t = low + i - b
+            held = sorted_ref[pl.ds(chunks + t, 1), :] == b.astype(f32)
+            row = jnp.where(held, sorted_ref[pl.ds(t, 1), :], -1.0)
+            columns = jnp.dot(
+                state_ref[:, pl.ds(b * TILE, TILE)], onehot(row, TILE), preferred_element_type=f32
+            ).reshape(members, levels, TILE)
+            dots_ref[start + i, :members] = jnp.sum(columns * wide[t][None], axis=1)
+            return carry
+
+        steps = high - low + buckets - 1
+        unroll = min(range(5, 9), key=lambda u: (steps % u, -u))
+        main = steps - steps % unroll
+        lax.fori_loop(0, main, pick, 0, unroll=unroll)
+        if main < steps:
+            lax.fori_loop(main, steps, pick, 0, unroll=steps - main)
+        if number == 1:
+            answer(1)
+        if number == 0:
+            for copy in passed:
+                copy.wait()
+            forward = started(
+                whole_wall(3), whole_wall(4), wall_send.at[4], wall_recv.at[4], cell=cell_of[1]
+            )
+
+    answer(2)
+    answer(0)
 
     for load in loads[5:]:
         load.wait()
@@ -521,7 +534,7 @@
     chunks = own + far * halo
     sources = 1 + far
     buckets = cell_dev // TILE
-    steps = chunks + 2 * (buckets - 1)
+    steps = chunks + 3 * (buckets - 1)
     share = obs_dev // sharers
     everyone = sharers * members
     width = everyone + 1 + (-(everyone + 1)) % 16

time: 37.4 us -> 36.7 us (0.981)
  Pallas kernels: 36.6 us -> 35.9 us
    pallas_call x1, Pallas kernels: 35.1 us -> 34.4 us  [on_device(): pl.pallas_call(functools.partial(kernel, own, halo), out_shape=jax.ShapeD...]
where the time goes in v3:
time: 36.7 us; the launch traced here: 36.5 us
  Pallas kernels  35.9 us (98%)
  between operations  0.64 us (2%)
    pallas_call x1, Pallas kernels, on_device(): pl.pallas_call(functools.partial(kernel, own, halo), out_shape=jax.ShapeD...  34.4 us
    pallas_call x1, Pallas kernels, on_device(): pl.pallas_call(functools.partial(unpack_kernel, everyone), out_shape=(jax...  1.43 us

profile of v3, /device:TPU:0, one launch (start us, length us, event | category | flops | bytes accessed | tf_op | source)
XLA Modules:
  0.0 36.5 jit_solution(13436291323677528847)
XLA Ops:
  0.6 34.4 %shard_map.95.final_ref = f32[40,96]{1,0:T(8,128)} custom-call(s32[16,1,256]{2,1,0:T(1,128)} %bitcast.13, s32[4,1024]{1,0:T(4,128)} %bitcast.14, f32[4,1024]{1,0:T(4,128)} %bitcast.15, bf16[120,1024]{1,0:T(8,128)(2,1)} %bitcast.12, bf16[1200,2048]{1,0:T(8,128)(2,1)} %bitcast.11, f32[1,1024]{1,0:T(1,128)} %bitcast.16, f32[1,1024]{1,0:T(1,128)} %bitcast.17, ...), custom_call_target="tpu_custom_call" | custom-call | tf_op jit(solution)/shard_map/pallas_call | solution.py:543
  35.1 1.4 %shard_map.96 = (f32[10,8,40]{2,1,0:T(8,128)}, f32[8,10]{1,0:T(8,128)}) custom-call(f32[40,96]{1,0:T(8,128)} %shard_map.95.final_ref), custom_call_target="tpu_custom_call" | custom-call | tf_op jit(solution)/shard_map/pallas_call | solution.py:594
